TPU v7x, 32 devices: a whole 2x2x4 slice. The times are simulated.
32 devices in a mesh: seq: 16 (over z, y, x), head: 2 (over core).
Axes of the slice: x: 2, y: 2, z: 4, core: 2. Of those that a mesh axis runs over, the one named last changes fastest.
Arguments:
- queries: bfloat16 [3072, 32, 128], P('seq', 'head'), may hold values from -180 to 180
- key_rows: bfloat16 [3072, 8, 128], P('seq', 'head'), may hold values from -4.5 to 4.5
- value_rows: bfloat16 [3072, 8, 128], P('seq', 'head'), may hold values from -24 to 24
- windows: int32 [32], P('head'), may hold values from 768 to 1536, as said below
- sink_counts: int32 [32], P('head'), may hold values from 1 to 4, as said below
- sink_bias: float32 [32], P('head'), may hold values from 3 to 7
- out_weight: bfloat16 [4096, 4096], P('head'), may hold values from -0.09375 to 0.09375
Outputs:
- attn_out: bfloat16 [3072, 4096], P(('seq', 'head'))
Inputs may be any that keep to these rules, and one draw needn't show every extreme that they name: `windows`: each head's window lies between 768 and 1536, and some head has exactly 1536. `sink_counts`: each head has 1 to 4 sink tokens, and some head has exactly 4.
All inputs are finite; a program needn't handle non-finite values.
Results may differ from a plain program's by a relative error of at most 0.018.
Values may be sent and summed in bfloat16 or wider, within the bound.
A program may use at most 128 MiB of HBM per device.

v0:
```python
import jax
import jax.numpy as jnp
from jax import lax
from jax.sharding import PartitionSpec as P

WINDOW = 1536
SINKS = 4


def shifted(block, axis, distance):
    devices = range(lax.axis_size(axis))
    route = [(i - distance, i) for i in devices if i - distance in devices]
    return lax.ppermute(block, axis, route)


def spread(value, axis, source):
    kept = jnp.where(lax.axis_index(axis) == source, value, 0).astype(value.dtype)
    return lax.psum(kept, axis)


def attend_block(query_block, band_rows, sink_rows, first_pos, windows, sink_counts, sink_bias):
    tok_rows, local_heads, head_width = query_block.shape
    kv_local = band_rows.shape[2]
    group_size = local_heads // kv_local
    band_span = band_rows.shape[1]
    sink_total = sink_rows.shape[1]
    all_keys = jnp.concatenate([sink_rows[0], band_rows[0]], axis=0)
    all_values = jnp.concatenate([sink_rows[1], band_rows[1]], axis=0)
    grouped = query_block.reshape(tok_rows, kv_local, group_size, head_width)
    score_scale = 1.0 / head_width**0.5
    scores = (
        jnp.einsum("tkgd,skd->kgts", grouped, all_keys, preferred_element_type=jnp.float32)
        * score_scale
    )
    query_pos = first_pos + jnp.arange(tok_rows, dtype=jnp.int32)
    band_pos = first_pos + tok_rows - band_span + jnp.arange(band_span, dtype=jnp.int32)
    sink_pos = jnp.arange(sink_total, dtype=jnp.int32)
    key_pos = jnp.concatenate([sink_pos, band_pos])
    is_sink = jnp.concatenate([jnp.ones((sink_total,), bool), jnp.zeros((band_span,), bool)])
    head_window = windows.reshape(kv_local, group_size, 1, 1)
    head_sinks = sink_counts.reshape(kv_local, group_size, 1, 1)
    head_bias = sink_bias.reshape(kv_local, group_size, 1, 1)
    distance = query_pos[:, None] - key_pos[None, :]
    visible = (distance >= 0) & jnp.where(
        is_sink, key_pos < head_sinks, (distance < head_window) & (key_pos >= head_sinks)
    )
    scores = scores + jnp.where(is_sink, head_bias, 0.0)
    masked = jnp.where(visible, scores, -1e30)
    highest = jnp.max(masked, axis=-1, keepdims=True)
    weights = jnp.where(visible, jnp.exp(masked - highest), 0.0)
    normed = (weights / jnp.sum(weights, axis=-1, keepdims=True)).astype(jnp.bfloat16)
    mixed = jnp.einsum("kgts,skd->tkgd", normed, all_values, preferred_element_type=jnp.float32)
    return mixed.astype(jnp.bfloat16).reshape(tok_rows, local_heads * head_width)


def shards(queries, key_rows, value_rows, windows, sink_counts, sink_bias, out_weight):
    tok_rows = queries.shape[0]
    stacked = jnp.stack([key_rows, value_rows])
    halo_depth = (WINDOW - 1) // tok_rows + 1
    received = [shifted(stacked, "seq", halo_depth - number) for number in range(halo_depth)]
    halo_rows = jnp.concatenate(received, axis=1)
    band_all = jnp.concatenate([halo_rows, stacked], axis=1)
    sink_rows = spread(stacked[:, :SINKS], "seq", 0)
    first_pos = lax.axis_index("seq") * tok_rows
    attended = attend_block(
        queries, band_all, sink_rows, first_pos, windows, sink_counts, sink_bias
    )
    return lax.psum_scatter(
        jnp.dot(attended, out_weight, preferred_element_type=jnp.float32).astype(jnp.bfloat16),
        "head",
        scatter_dimension=0,
        tiled=True,
    )


def solution(mesh):
    in_specs = (
        P("seq", "head", None),
        P("seq", "head", None),
        P("seq", "head", None),
        P("head"),
        P("head"),
        P("head"),
        P("head", None),
    )
    out_specs = P(("seq", "head"), None)
    return jax.shard_map(shards, mesh=mesh, in_specs=in_specs, out_specs=out_specs, check_vma=False)
```

profile of v0, /device:TPU:17, one launch (start us, length us, event | category | flops | bytes accessed | tf_op | source)
XLA Modules:
  0.0 205.7 jit_solution(545283208927438554)
XLA Ops:
  6.5 1.1 copy_bitcast_fusion
  7.7 3.1 %collective-permute-start.6 = (bf16[2,192,4,128]{3,1,2,0:T(8,128)(2,1)S(1)}, bf16[2,192,4,128]{3,1,2,0:T(8,128)(2,1)S(1)}, u32[]{:S(2)}, u32[]{:S(2)}) collective-permute-start(bf16[2,192,4,128]{3,1,2,0:T(8,128)(2,1)S(1)} %pad_maximum_fusion), channel_id=1, source_target_pairs={{0,4},{2,6},{4,8},{6,10},{8,12},{10,14},{12,16},{14,18},{16,20},{1... | collective-permute-start | bytes 1179656 | tf_op jit(solution)/shard_map/ppermute | solution.py:13
  10.9 4.1 %collective-permute-start.3 = (bf16[2,192,4,128]{3,1,2,0:T(8,128)(2,1)S(1)}, bf16[2,192,4,128]{3,1,2,0:T(8,128)(2,1)S(1)}, u32[]{:S(2)}, u32[]{:S(2)}) collective-permute-start(bf16[2,192,4,128]{3,1,2,0:T(8,128)(2,1)S(1)} %pad_maximum_fusion), channel_id=1, source_target_pairs={{0,10},{2,12},{4,14},{6,16},{8,18},{10,20},{12,22},{14,24},{16,26}... | collective-permute-start | bytes 1179656 | tf_op jit(solution)/shard_map/ppermute | solution.py:13
  15.0 1.9 collective-permute-start.2
  17.0 1.9 collective-permute-start.1
  18.9 1.3 collective-permute-start
  20.2 0.1 pad_add_fusion
  20.3 1.0 broadcast_compare_fusion
  21.3 1.3 broadcast_subtract_fusion
  22.6 0.7 lt.36
  23.3 0.7 broadcast_in_dim.53
  24.1 1.4 broadcast_select_fusion
  25.5 0.8 broadcast_compare_fusion.2
  26.3 89.4 %psum.7 = bf16[2,4,4,128]{3,1,2,0:T(4,128)(2,1)S(1)} all-reduce(bf16[2,4,4,128]{3,1,2,0:T(4,128)(2,1)S(1)} %fusion.29), channel_id=1, replica_groups=mesh['seq'=16,'head'=2] {'seq'}, use_global_device_ids=true, to_apply=%region_0.1 | all-reduce | flops 4096 | bytes 16384 | tf_op jit(solution)/shard_map/psum | solution.py:18
  115.6 0.7 lt.40
  116.4 0.0 collective-permute-done
  116.4 1.9 collective-permute-start.4
  118.3 0.0 collective-permute-done.1
  118.3 3.0 %collective-permute-start.5 = (bf16[2,192,4,128]{3,1,2,0:T(8,128)(2,1)S(1)}, bf16[2,192,4,128]{3,1,2,0:T(8,128)(2,1)S(1)}, u32[]{:S(2)}, u32[]{:S(2)}) collective-permute-start(bf16[2,192,4,128]{3,1,2,0:T(8,128)(2,1)S(1)} %pad_maximum_fusion), channel_id=1, source_target_pairs={{0,6},{2,8},{4,10},{6,12},{8,14},{10,16},{12,18},{14,20},{16,22},{... | collective-permute-start | bytes 1179656 | tf_op jit(solution)/shard_map/ppermute | solution.py:13
  121.4 0.1 constant_dynamic-update-slice_fusion.7
  121.4 0.0 collective-permute-done.2
  121.4 2.5 %collective-permute-start.7 = (bf16[2,192,4,128]{3,1,2,0:T(8,128)(2,1)S(1)}, bf16[2,192,4,128]{3,1,2,0:T(8,128)(2,1)S(1)}, u32[]{:S(2)}, u32[]{:S(2)}) collective-permute-start(bf16[2,192,4,128]{3,1,2,0:T(8,128)(2,1)S(1)} %pad_maximum_fusion), channel_id=1, source_target_pairs={{0,2},{2,4},{4,6},{6,8},{8,10},{10,12},{12,14},{14,16},{16,18},{18... | collective-permute-start | bytes 1179656 | tf_op jit(solution)/shard_map/ppermute | solution.py:13
  124.0 0.1 constant_dynamic-update-slice_fusion.6
  124.0 0.0 collective-permute-done.3
  124.0 0.1 constant_dynamic-update-slice_fusion.5
  124.1 0.8 collective-permute-done.4
  124.9 0.1 constant_dynamic-update-slice_fusion.4
  125.0 5.7 %collective-permute-done.5 = bf16[2,192,4,128]{3,1,2,0:T(8,128)(2,1)S(1)} collective-permute-done((bf16[2,192,4,128]{3,1,2,0:T(8,128)(2,1)S(1)}, bf16[2,192,4,128]{3,1,2,0:T(8,128)(2,1)S(1)}, u32[]{:S(2)}, u32[]{:S(2)}) %collective-permute-start.5) | collective-permute-done | bytes 393248 | tf_op jit(solution)/shard_map/ppermute | solution.py:13
  130.6 0.1 constant_dynamic-update-slice_fusion.3
  130.7 0.0 collective-permute-done.6
  130.7 0.1 constant_dynamic-update-slice_fusion.2
  130.8 7.9 %collective-permute-done.7 = bf16[2,192,4,128]{3,1,2,0:T(8,128)(2,1)S(1)} collective-permute-done((bf16[2,192,4,128]{3,1,2,0:T(8,128)(2,1)S(1)}, bf16[2,192,4,128]{3,1,2,0:T(8,128)(2,1)S(1)}, u32[]{:S(2)}, u32[]{:S(2)}) %collective-permute-start.7) | collective-permute-done | bytes 393248 | tf_op jit(solution)/shard_map/ppermute | solution.py:13
  138.6 0.1 constant_dynamic-update-slice_fusion.1
  138.7 0.1 constant_dynamic-update-slice_fusion
  138.7 0.0 copy-start.1
  138.7 0.0 copy-start.2
  138.8 0.0 copy-start.3
  138.8 0.0 copy-start.4
  138.8 0.0 copy-start.5
  138.8 1.5 slice_bitcast_fusion.1
  140.3 0.0 copy-done.1
  140.3 21.8 %fusion.36 = (f32[4,4,192]{2,1,0:T(4,128)S(1)}, f32[4,4,192,1732]{3,2,1,0:T(8,128)}) fusion(f32[4,4,1732]{2,1,0:T(4,128)S(1)} %copy-done.2, s32[4,4]{1,0:T(4,128)S(1)} %lt.40, s32[192,1732]{1,0:T(8,128)} %broadcast_subtract_fusion, pred[4,4,1732]{2,1,0:T(4,128)(4,1)S(1)} %copy-done.4, pred[4,4,1732]{2,1,0:T(4,128)(4,1)S(1)} %copy-done.3, ...), kind=kOutput, calls=%fused_computation.64 | convolution fusion | flops 1440139008 | bytes 25685892 | tf_op jit(solution)/shard_map/sub | solution.py:50
  162.1 8.9 %fusion.24 = bf16[192,4,4,128]{3,0,2,1:T(8,128)(2,1)S(1)} fusion(f32[4,4,192,1732]{3,2,1,0:T(8,128)} %get-tuple-element.12, f32[4,4,192]{2,1,0:T(4,128)S(1)} %get-tuple-element.11, bf16[1728,4,128]{2,0,1:T(8,128)(2,1)S(1)} %get-tuple-element.5, bf16[4,4,128]{2,0,1:T(4,128)(2,1)S(1)} %get-tuple-element.9), kind=kOutput, calls=%fused_computation.30 | convolution fusion | flops 1376681984 | bytes 23855104 | tf_op jit(solution)/shard_map/kgts,skd->tkgd/dot_general | solution.py:52
  171.0 0.6 copy.14
  171.6 0.6 reshape.86
  172.2 10.3 %convolution_convert_fusion = bf16[192,4096]{1,0:T(8,128)(2,1)} fusion(bf16[192,2048]{1,0:T(8,128)(2,1)S(1)} %reshape.86, bf16[2048,4096]{1,0:T(8,128)(2,1)} %param.13), kind=kOutput, calls=%fused_computation.17 | convolution fusion | flops 3222011904 | bytes 19136512 | tf_op jit(solution)/shard_map/dot_general | solution.py:69
  182.6 0.0 reduce-scatter.2.cloned.1.call-update
  182.6 16.3 %reduce-scatter.2.cloned.1.call-done = bf16[96,4096]{1,0:T(8,128)(2,1)} async-done(((bf16[192,4096]{1,0:T(8,128)(2,1)}), bf16[96,4096]{1,0:T(8,128)(2,1)}) %reduce-scatter.2.cloned.1.call-update) | async-done | bytes 786448 | tf_op jit(solution)/shard_map/reduce_scatter | solution.py:68
  (14 shorter events, 0.1 us)
Async XLA Ops:
  6.5 133.7 %copy-start = (bf16[192,16,128]{2,1,0:T(8,128)(2,1)S(1)}, bf16[192,16,128]{2,1,0:T(8,128)(2,1)}, u32[]{:S(2)}) copy-start(bf16[192,16,128]{2,1,0:T(8,128)(2,1)} %param.7) | copy-start | bytes 2359300
  6.5 192.3 %reduce-scatter.2.cloned.1.call-start = ((), (), s32[]{:S(2)}) async-start(), calls=%async_computation.1 | async-start | bytes 2359296 | tf_op jit(solution)/shard_map/reduce_scatter | solution.py:68
  7.7 123.0 %collective-permute-start.6 = (bf16[2,192,4,128]{3,1,2,0:T(8,128)(2,1)S(1)}, bf16[2,192,4,128]{3,1,2,0:T(8,128)(2,1)S(1)}, u32[]{:S(2)}, u32[]{:S(2)}) collective-permute-start(bf16[2,192,4,128]{3,1,2,0:T(8,128)(2,1)S(1)} %pad_maximum_fusion), channel_id=1, source_target_pairs={{0,4},{2,6},{4,8},{6,10},{8,12},{10,14},{12,16},{14,18},{16,20},{1... | collective-permute-start | bytes 1179656 | tf_op jit(solution)/shard_map/ppermute | solution.py:13
  10.9 113.1 %collective-permute-start.3 = (bf16[2,192,4,128]{3,1,2,0:T(8,128)(2,1)S(1)}, bf16[2,192,4,128]{3,1,2,0:T(8,128)(2,1)S(1)}, u32[]{:S(2)}, u32[]{:S(2)}) collective-permute-start(bf16[2,192,4,128]{3,1,2,0:T(8,128)(2,1)S(1)} %pad_maximum_fusion), channel_id=1, source_target_pairs={{0,10},{2,12},{4,14},{6,16},{8,18},{10,20},{12,22},{14,24},{16,26}... | collective-permute-start | bytes 1179656 | tf_op jit(solution)/shard_map/ppermute | solution.py:13
  15.0 106.4 %collective-permute-start.2 = (bf16[2,192,4,128]{3,1,2,0:T(8,128)(2,1)S(1)}, bf16[2,192,4,128]{3,1,2,0:T(8,128)(2,1)S(1)}, u32[]{:S(2)}, u32[]{:S(2)}) collective-permute-start(bf16[2,192,4,128]{3,1,2,0:T(8,128)(2,1)S(1)} %pad_maximum_fusion), channel_id=1, source_target_pairs={{0,12},{2,14},{4,16},{6,18},{8,20},{10,22},{12,24},{14,26},{16,28}... | collective-permute-start | bytes 1179656 | tf_op jit(solution)/shard_map/ppermute | solution.py:13
  17.0 101.4 %collective-permute-start.1 = (bf16[2,192,4,128]{3,1,2,0:T(8,128)(2,1)S(1)}, bf16[2,192,4,128]{3,1,2,0:T(8,128)(2,1)S(1)}, u32[]{:S(2)}, u32[]{:S(2)}) collective-permute-start(bf16[2,192,4,128]{3,1,2,0:T(8,128)(2,1)S(1)} %pad_maximum_fusion), channel_id=1, source_target_pairs={{0,14},{2,16},{4,18},{6,20},{8,22},{10,24},{12,26},{14,28},{16,30}... | collective-permute-start | bytes 1179656 | tf_op jit(solution)/shard_map/ppermute | solution.py:13
  18.9 97.5 %collective-permute-start = (bf16[2,192,4,128]{3,1,2,0:T(8,128)(2,1)S(1)}, bf16[2,192,4,128]{3,1,2,0:T(8,128)(2,1)S(1)}, u32[]{:S(2)}, u32[]{:S(2)}) collective-permute-start(bf16[2,192,4,128]{3,1,2,0:T(8,128)(2,1)S(1)} %pad_maximum_fusion), channel_id=1, source_target_pairs={{0,16},{2,18},{4,20},{6,22},{8,24},{10,26},{12,28},{14,30},{1,17},... | collective-permute-start | bytes 1179656 | tf_op jit(solution)/shard_map/ppermute | solution.py:13
  116.4 8.5 %collective-permute-start.4 = (bf16[2,192,4,128]{3,1,2,0:T(8,128)(2,1)S(1)}, bf16[2,192,4,128]{3,1,2,0:T(8,128)(2,1)S(1)}, u32[]{:S(2)}, u32[]{:S(2)}) collective-permute-start(bf16[2,192,4,128]{3,1,2,0:T(8,128)(2,1)S(1)} %pad_maximum_fusion), channel_id=1, source_target_pairs={{0,8},{2,10},{4,12},{6,14},{8,16},{10,18},{12,20},{14,22},{16,24},... | collective-permute-start | bytes 1179656 | tf_op jit(solution)/shard_map/ppermute | solution.py:13
  118.3 12.3 %collective-permute-start.5 = (bf16[2,192,4,128]{3,1,2,0:T(8,128)(2,1)S(1)}, bf16[2,192,4,128]{3,1,2,0:T(8,128)(2,1)S(1)}, u32[]{:S(2)}, u32[]{:S(2)}) collective-permute-start(bf16[2,192,4,128]{3,1,2,0:T(8,128)(2,1)S(1)} %pad_maximum_fusion), channel_id=1, source_target_pairs={{0,6},{2,8},{4,10},{6,12},{8,14},{10,16},{12,18},{14,20},{16,22},{... | collective-permute-start | bytes 1179656 | tf_op jit(solution)/shard_map/ppermute | solution.py:13
  121.4 17.2 %collective-permute-start.7 = (bf16[2,192,4,128]{3,1,2,0:T(8,128)(2,1)S(1)}, bf16[2,192,4,128]{3,1,2,0:T(8,128)(2,1)S(1)}, u32[]{:S(2)}, u32[]{:S(2)}) collective-permute-start(bf16[2,192,4,128]{3,1,2,0:T(8,128)(2,1)S(1)} %pad_maximum_fusion), channel_id=1, source_target_pairs={{0,2},{2,4},{4,6},{6,8},{8,10},{10,12},{12,14},{14,16},{16,18},{18... | collective-permute-start | bytes 1179656 | tf_op jit(solution)/shard_map/ppermute | solution.py:13
  138.7 1.5 copy-start.1
  138.7 1.5 copy-start.2
  138.8 1.5 copy-start.3
  138.8 1.5 copy-start.4
  138.8 1.5 copy-start.5
Sparse Core Ops, SparseCore 0:
  182.7 16.1 reduce-scatter.1
where the time goes:
time: 207 us; the launch traced here: 206 us
  blocking collectives  89.4 us (43%)
  matrix products  41.1 us (20%)
  waiting for transfers between devices  30.6 us (15%)
  starting transfers between devices  19.9 us (10%)
  between operations  13.7 us (7%)
  local copies, waits for them, and re-layouts  6.47 us (3%)
  other arithmetic  4.65 us (2%)
    psum x1, blocking collectives, spread(): return lax.psum(kept, axis)  89.4 us
    sub x1, matrix products, attend_block(): weights = jnp.where(visible, jnp.exp(masked - highest), 0.0)  21.8 us
    ppermute x8, starting transfers between devices, shifted(): return lax.ppermute(block, axis, route)  19.9 us
    reduce_scatter x1, waiting for transfers between devices, shards(): lax.psum_scatter(jnp.dot(attended, out_weight, preferred_element_type=jnp...  16.3 us
    ppermute x8, waiting for transfers between devices, shifted(): return lax.ppermute(block, axis, route)  14.3 us
    dot_general x1, matrix products, shards(): jnp.dot(attended, out_weight, preferred_element_type=jnp.float32)  10.3 us
    dot_general x1, matrix products, attend_block(): jnp.einsum('kgts,skd->tkgd', normed, all_values, preferred_element_type=j...  8.91 us
  transfers between devices with their start and end apart: 9, of which 4 were waited for; matrix products, arithmetic and copies ran while one was open for 3% of the time, Pallas kernels for 0%

commit v1 on v0

v1 whole, which is shorter than its diff:
```python
import functools

import jax
import jax.numpy as jnp
from jax import lax
from jax.experimental import pallas as pl
from jax.experimental.pallas import tpu as pltpu
from jax.sharding import PartitionSpec as P

WINDOW = 1536
SINKS = 4
PLANE = 4
SINK_ROWS = 16
HIDDEN = -1e30
LOG2E = 1.4426950408889634
MESH = pl.DeviceIdType.MESH


def kernel(
    n_seq, n_head, tile,
    win_ref, cnt_ref, bias_ref, own, q_ref, w_hbm, out_ref,
    kv, sink, qt, low, few, lift, top, norm, acc, att, w, part, got,
    send_sem, recv_sem, sink_send, sink_recv, w_sem, part_send, part_recv,
):
    me, side = lax.axis_index("seq"), lax.axis_index("head")
    heads_kv, _, rows, width = own.shape
    lanes = q_ref.shape[1]
    group = lanes // rows
    model = w.shape[1]
    share = rows // n_head
    z, p = me // PLANE, lax.rem(me, PLANE)
    bit0, bit1 = lax.rem(p, 2), p // 2
    px, py = p + 1 - 2 * bit0, p + 2 - 4 * bit1
    pd = 3 - p
    base = z * PLANE
    n_z = n_seq // PLANE
    scale = LOG2E / width**0.5

    barrier = pltpu.get_barrier_semaphore()

    def greet(axis, here, count):
        def one(step, carry):
            pl.semaphore_signal(
                barrier, inc=1, device_id={axis: lax.rem(here + step, count)}, device_id_type=MESH
            )
            return carry
        lax.fori_loop(1, count, one, 0)

    greet("seq", me, n_seq)
    greet("head", side, n_head)
    pl.semaphore_wait(barrier, n_seq + n_head - 2)

    def send(kind, src, plane, source, c, target):
        return pltpu.make_async_remote_copy(
            src_ref=src,
            dst_ref=kv.at[plane * PLANE + source, c],
            send_sem=send_sem.at[kind, c],
            recv_sem=recv_sem.at[plane * PLANE + source, c],
            device_id={"seq": target},
            device_id_type=MESH,
        )

    def landed(plane, source, c):
        send(0, own.at[c], plane, source, c, me).wait_recv()

    def held(plane, source, c):
        return kv.at[plane * PLANE + source, c]

    x_old, y_old, d_old = 2 * bit0, 2 * bit1, 2 * bit1
    x_from, y_from, d_from = 2 - 2 * bit0, 2 - 2 * bit1, 2 - 2 * bit1

    def sink_copy(target):
        return pltpu.make_async_remote_copy(
            src_ref=own.at[:, :, pl.ds(0, SINK_ROWS)],
            dst_ref=sink,
            send_sem=sink_send.at[target],
            recv_sem=sink_recv,
            device_id={"seq": target},
            device_id_type=MESH,
        )

    for c in range(heads_kv):
        @pl.when(z + 1 < n_z)
        def _():
            send(0, own.at[c], 1, p, c, me + PLANE).start()

        @pl.when(x_old == 0)
        def _():
            send(2, own.at[c], 0, p, c, base + px).start()

        @pl.when(y_old == 0)
        def _():
            send(3, own.at[c], 0, p, c, base + py).start()

        if c == 0:
            @pl.when(me == 0)
            def _():
                def one(target, carry):
                    sink_copy(target).start()
                    return carry
                lax.fori_loop(1, n_seq, one, 0)

    fetch = pltpu.make_async_copy(w_hbm, w, w_sem)
    fetch.start()

    column = lax.broadcasted_iota(jnp.int32, (1, lanes), 1)
    for c in range(heads_kv):
        window, count, bias, token = (jnp.zeros((1, lanes), t) for t in (jnp.int32, jnp.int32, jnp.float32, jnp.int32))
        for g in range(group):
            mine = (column >= g * rows) & (column < (g + 1) * rows)
            h = c * group + g
            window = jnp.where(mine, win_ref[h], window)
            count = jnp.where(mine, cnt_ref[h], count)
            bias = jnp.where(mine, bias_ref[h], bias)
            token = jnp.where(mine, column - g * rows, token)
        token = token + me * rows
        low[c] = jnp.maximum(token - window, count - 1)
        few[c] = jnp.minimum(token, count - 1)
        lift[c] = bias * LOG2E
        qt[c] = q_ref[c].T
        top[c] = jnp.full((1, lanes), HIDDEN, jnp.float32)
        norm[c] = jnp.zeros((1, lanes), jnp.float32)
        acc[c] = jnp.zeros((width, lanes), jnp.float32)

    def attend(block, c, shard, causal=False, sinks=False):
        keys, values = block[0], block[1]
        key_row = lax.broadcasted_iota(jnp.int32, (keys.shape[0], 1), 0)
        for n in range(0, lanes, 256):
            cols = slice(n, n + 256)
            s = jnp.dot(keys, qt[c, :, cols], preferred_element_type=jnp.float32) * scale
            if sinks:
                s = jnp.where(key_row <= few[c, :, cols], s + lift[c, :, cols], HIDDEN)
            else:
                seen = key_row > low[c, :, cols] - shard * rows
                if causal:
                    token = lax.rem(lax.broadcasted_iota(jnp.int32, (1, 256), 1) + n, rows)
                    seen = seen & (key_row <= token)
                s = jnp.where(seen, s, HIDDEN)
            old = top[c, :, cols]
            new = jnp.maximum(old, jnp.max(s, axis=0, keepdims=True))
            e = jnp.exp2(s - new)
            fade = jnp.exp2(old - new)
            top[c, :, cols] = new
            norm[c, :, cols] = norm[c, :, cols] * fade + jnp.sum(e, axis=0, keepdims=True)
            acc[c, :, cols] = acc[c, :, cols] * fade + lax.dot_general(
                values, e.astype(jnp.bfloat16), (((0,), (0,)), ((), ())),
                preferred_element_type=jnp.float32,
            )

    def each(body):
        def one(c, carry):
            body(c)
            return carry
        lax.fori_loop(0, heads_kv, one, 0)

    each(lambda c: attend(own.at[c], c, me, causal=True))

    @pl.when(z >= 1)
    def _():
        def first(c):
            landed(1, p, c)

            @pl.when(z + 1 < n_z)
            def _():
                send(1, held(1, p, c), 2, p, c, me + PLANE).start()

            send(4, held(1, p, c), 1, p, c, base + px).start()
            send(5, held(1, p, c), 1, p, c, base + py).start()
            attend(held(1, p, c), c, me - PLANE)
        each(first)

        def second(c):
            @pl.when(z >= 2)
            def _():
                landed(2, p, c)

                @pl.when(x_old == 2)
                def _():
                    send(2, held(2, p, c), 2, p, c, base + px).start()

                @pl.when(y_old == 2)
                def _():
                    send(3, held(2, p, c), 2, p, c, base + py).start()

            landed(1, px, c)
            send(6, held(1, px, c), 1, px, c, base + py).start()
            attend(held(1, px, c), c, base - PLANE + px)
        each(second)

    def relay(c):
        @pl.when(z >= y_from)
        def _():
            landed(y_from, py, c)
            send(7, held(y_from, py, c), y_from, py, c, base + px).start()
            attend(held(y_from, py, c), c, base - y_from * PLANE + py)
    each(relay)

    @pl.when(me == 0)
    def _():
        each(lambda c: attend(own.at[c, :, pl.ds(0, SINK_ROWS)], c, 0, sinks=True))

    @pl.when(me > 0)
    def _():
        sink_copy(me).wait_recv()
        each(lambda c: attend(sink.at[c], c, 0, sinks=True))

    @pl.when(z >= 2)
    def _():
        each(lambda c: attend(held(2, p, c), c, me - 2 * PLANE))

    @pl.when(z >= 1)
    def _():
        def third(c):
            landed(1, py, c)
            attend(held(1, py, c), c, base - PLANE + py)
        each(third)

    @pl.when(z >= x_from)
    def _():
        def fourth(c):
            landed(x_from, px, c)
            attend(held(x_from, px, c), c, base - x_from * PLANE + px)
        each(fourth)

    @pl.when(z >= 1)
    def _():
        def fifth(c):
            landed(1, pd, c)
            attend(held(1, pd, c), c, base - PLANE + pd)
        each(fifth)

    @pl.when(z >= d_from)
    def _():
        def sixth(c):
            landed(d_from, pd, c)
            attend(held(d_from, pd, c), c, base - d_from * PLANE + pd)
        each(sixth)

    for c in range(heads_kv):
        mixed = (acc[c] / norm[c]).T.astype(jnp.bfloat16)
        for g in range(group):
            h = c * group + g
            att[:, h * width:(h + 1) * width] = mixed[g * rows:(g + 1) * rows]

    fetch.wait()
    tiles = model // tile

    def give(t, step):
        target = lax.rem(side + step, n_head)
        return pltpu.make_async_remote_copy(
            src_ref=part.at[t, target],
            dst_ref=got.at[t, step - 1],
            send_sem=part_send.at[t, step - 1],
            recv_sem=part_recv.at[t, step - 1],
            device_id={"head": target},
            device_id_type=MESH,
        )

    def project(t, carry):
        cols = pl.ds(pl.multiple_of(t * tile, tile), tile)
        total = jnp.dot(att[...], w[:, cols], preferred_element_type=jnp.float32)
        for d in range(n_head):
            part[t, d] = total[d * share:(d + 1) * share].astype(jnp.bfloat16)

        @pl.when(t >= 1)
        def _():
            for step in range(1, n_head):
                give(t - 1, step).start()
        return carry
    lax.fori_loop(0, tiles, project, 0)
    for step in range(1, n_head):
        give(tiles - 1, step).start()

    def finish(t, carry):
        total = part[t, side].astype(jnp.float32)
        for step in range(1, n_head):
            give(t, step).wait_recv()
            total = total + got[t, step - 1].astype(jnp.float32)
        out_ref[:, pl.ds(pl.multiple_of(t * tile, tile), tile)] = total.astype(jnp.bfloat16)
        return carry
    lax.fori_loop(0, tiles, finish, 0)

    def sent(kind, plane, source, c, target):
        send(kind, held(plane, source, c), plane, source, c, target).wait_send()

    def drain(c):
        @pl.when(z + 1 < n_z)
        def _():
            sent(0, 1, p, c, me + PLANE)

        @pl.when(z >= x_old)
        def _():
            sent(2, x_old, p, c, base + px)

        @pl.when(z >= y_old)
        def _():
            sent(3, y_old, p, c, base + py)

        @pl.when(z >= 1)
        def _():
            @pl.when(z + 1 < n_z)
            def _():
                sent(1, 2, p, c, me + PLANE)
            sent(4, 1, p, c, base + px)
            sent(5, 1, p, c, base + py)
            sent(6, 1, px, c, base + py)

        @pl.when(z >= y_from)
        def _():
            sent(7, y_from, py, c, base + px)
    each(drain)

    @pl.when(me == 0)
    def _():
        def one(target, carry):
            sink_copy(target).wait_send()
            return carry
        lax.fori_loop(1, n_seq, one, 0)

    def gone(t, carry):
        for step in range(1, n_head):
            give(t, step).wait_send()
        return carry
    lax.fori_loop(0, tiles, gone, 0)


def shards(n_seq, n_head, queries, key_rows, value_rows, windows, sink_counts, sink_bias, out_weight):
    rows, heads, width = queries.shape
    kv_heads = key_rows.shape[1]
    group = heads // kv_heads
    lanes = group * rows
    depth, model = out_weight.shape
    assert (WINDOW - 1) // rows + 1 == 2 * PLANE and n_seq % PLANE == 0
    own = jnp.stack([key_rows, value_rows]).transpose(2, 0, 1, 3)
    q = queries.transpose(1, 0, 2).reshape(kv_heads, lanes, width)
    tile = min(512, model)
    tiles = model // tile
    share = rows // n_head
    bf16, f32, i32 = jnp.bfloat16, jnp.float32, jnp.int32
    vmem = pl.BlockSpec(memory_space=pltpu.VMEM)
    smem = pl.BlockSpec(memory_space=pltpu.SMEM)
    dma = pltpu.SemaphoreType.DMA
    return pl.pallas_call(
        functools.partial(kernel, n_seq, n_head, tile),
        out_shape=jax.ShapeDtypeStruct((share, model), bf16),
        in_specs=[smem, smem, smem, vmem, vmem, pl.BlockSpec(memory_space=pl.ANY)],
        out_specs=vmem,
        scratch_shapes=[
            pltpu.VMEM((3 * PLANE, kv_heads, 2, rows, width), bf16),
            pltpu.VMEM((kv_heads, 2, SINK_ROWS, width), bf16),
            pltpu.VMEM((kv_heads, width, lanes), bf16),
            pltpu.VMEM((kv_heads, 1, lanes), i32),
            pltpu.VMEM((kv_heads, 1, lanes), i32),
            pltpu.VMEM((kv_heads, 1, lanes), f32),
            pltpu.VMEM((kv_heads, 1, lanes), f32),
            pltpu.VMEM((kv_heads, 1, lanes), f32),
            pltpu.VMEM((kv_heads, width, lanes), f32),
            pltpu.VMEM((rows, depth), bf16),
            pltpu.VMEM((depth, model), bf16),
            pltpu.VMEM((tiles, n_head, share, tile), bf16),
            pltpu.VMEM((tiles, n_head - 1, share, tile), bf16),
            dma((8, kv_heads)),
            dma((3 * PLANE, kv_heads)),
            dma((n_seq,)),
            dma,
            dma,
            dma((tiles, n_head - 1)),
            dma((tiles, n_head - 1)),
        ],
        compiler_params=pltpu.CompilerParams(
            collective_id=0, has_side_effects=True, vmem_limit_bytes=56 * 1024 * 1024
        ),
    )(windows, sink_counts, sink_bias, own, q, out_weight)


def solution(mesh):
    in_specs = (
        P("seq", "head", None),
        P("seq", "head", None),
        P("seq", "head", None),
        P("head"),
        P("head"),
        P("head"),
        P("head", None),
    )
    body = functools.partial(shards, mesh.shape["seq"], mesh.shape["head"])
    out_specs = P(("seq", "head"), None)
    return jax.shard_map(body, mesh=mesh, in_specs=in_specs, out_specs=out_specs, check_vma=False)
```

time: 207 us -> 70.9 us (0.34)
  blocking collectives: 89.4 us -> 0 us
  Pallas kernels: 0 us -> 64.5 us
  matrix products: 41.1 us -> 0 us
  waiting for transfers between devices: 30.6 us -> 0 us
  starting transfers between devices: 19.9 us -> 0 us
  between operations: 13.7 us -> 0.01 us
  other arithmetic: 4.65 us -> 0.78 us
    psum x1 -> x0, blocking collectives: 89.4 us -> none  [spread(): return lax.psum(kept, axis)]
    pallas_call x0 -> x1, Pallas kernels: none -> 64.5 us  [shards(): pl.pallas_call(functools.partial(kernel, n_seq, n_head, tile), out_shape=...]
    sub x1 -> x0, matrix products: 21.8 us -> none  [attend_block(): weights = jnp.where(visible, jnp.exp(masked - highest), 0.0)]
    ppermute x8 -> x0, starting transfers between devices: 19.9 us -> none  [shifted(): return lax.ppermute(block, axis, route)]
    dot_general x2 -> x0, matrix products: 19.3 us -> none  [the longest x1 10.3 us: shards(): jnp.dot(attended, out_weight, preferred_element_type=jnp.float32)]
    reduce_scatter x1 -> x0, waiting for transfers between devices: 16.3 us -> none  [shards(): lax.psum_scatter(jnp.dot(attended, out_weight, preferred_element_type=jnp...]
    ppermute x8 -> x0, waiting for transfers between devices: 14.3 us -> none  [shifted(): return lax.ppermute(block, axis, route)]
    transpose x0 -> x1, local copies, waits for them, and re-layouts: none -> 2.22 us  [shards(): q = queries.transpose(1, 0, 2).reshape(kv_heads, lanes, width)]
  transfers between devices with their start and end apart: 9 -> 0, of which waited for: 4 -> 0; matrix products, arithmetic and copies ran while one was open for 3% -> 0% of each run, Pallas kernels for 0% -> 0%
where the time goes in v1:
time: 70.9 us; the launch traced here: 70.7 us
  Pallas kernels  64.5 us (91%)
  local copies, waits for them, and re-layouts  5.35 us (8%)
  other arithmetic  0.78 us (1%)
    pallas_call x1, Pallas kernels, shards(): pl.pallas_call(functools.partial(kernel, n_seq, n_head, tile), out_shape=...  64.5 us
    transpose x1, local copies, waits for them, and re-layouts, shards(): q = queries.transpose(1, 0, 2).reshape(kv_heads, lanes, width)  2.22 us
    unnamed x1, local copies, waits for them, and re-layouts  2.06 us

profile of v1, /device:TPU:17, one launch (start us, length us, event | category | flops | bytes accessed | tf_op | source)
XLA Modules:
  0.0 70.7 jit_solution(7987483223042751810)
XLA Ops:
  0.0 1.1 %copy_bitcast_fusion = (bf16[1,192,4,128]{3,1,0,2:T(8,128)(2,1)S(1)}, bf16[1,192,4,128]{3,1,0,2:T(8,128)(2,1)S(1)}) fusion(bf16[192,4,128]{2,1,0:T(4,128)(2,1)} %param.9, bf16[192,4,128]{2,1,0:T(4,128)(2,1)} %param.8), kind=kLoop, calls=%fused_computation.1 | loop fusion | bytes 786432 | tf_op jit(solution)/shard_map/stack | solution.py:334
  1.1 0.8 %maximum_bitcast_fusion.own = bf16[4,2,192,128]{3,2,1,0:T(8,128)(2,1)} fusion(bf16[1,192,4,128]{3,1,0,2:T(8,128)(2,1)S(1)} %get-tuple-element.5, bf16[1,192,4,128]{3,1,0,2:T(8,128)(2,1)S(1)} %get-tuple-element.6), kind=kLoop, calls=%fused_computation | loop fusion | flops 196608 | bytes 786432 | tf_op jit(solution)/shard_map/transpose | solution.py:334
  1.9 2.2 %copy.10 = bf16[16,192,128]{2,1,0:T(8,128)(2,1)} copy(bf16[16,192,128]{2,0,1:T(8,128)(2,1)} %bitcast.9) | data formatting | bytes 1572864 | tf_op jit(solution)/shard_map/transpose | solution.py:335
  4.1 64.5 %shard_map.73 = bf16[96,4096]{1,0:T(8,128)(2,1)} custom-call(s32[16]{0:T(128)} %win_ref.1, s32[16]{0:T(128)} %cnt_ref.1, f32[16]{0:T(128)} %bias_ref.1, bf16[4,2,192,128]{3,2,1,0:T(8,128)(2,1)} %maximum_bitcast_fusion.own, bf16[4,768,128]{2,1,0:T(8,128)(2,1)} %bitcast.8, bf16[2048,4096]{1,0:T(8,128)(2,1)} %w_hbm.1), custom_call_target="tpu_custom_call" | custom-call | tf_op jit(solution)/shard_map/pallas_call | solution.py:343
  68.6 2.1 %copy.14 = bf16[96,4096]{1,0:T(8,128)(2,1)} copy(bf16[96,4096]{1,0:T(8,128)(2,1)} %shard_map.73) | data formatting | bytes 1572864

commit v2 on v1

--- a/solution.py
+++ b/solution.py
@@ -18,9 +18,9 @@
 
 def kernel(
     n_seq, n_head, tile,
-    win_ref, cnt_ref, bias_ref, own, q_ref, w_hbm, out_ref,
-    kv, sink, qt, low, few, lift, top, norm, acc, att, w, part, got,
-    send_sem, recv_sem, sink_send, sink_recv, w_sem, part_send, part_recv,
+    win_ref, cnt_ref, bias_ref, k_hbm, v_hbm, q_hbm, w_hbm, out_ref,
+    own, q_ref, kv, sink, qt, low, few, lift, top, norm, acc, att, w, part, got,
+    send_sem, recv_sem, sink_send, sink_recv, own_sem, q_sem, w_sem, part_send, part_recv,
 ):
     me, side = lax.axis_index("seq"), lax.axis_index("head")
     heads_kv, _, rows, width = own.shape
@@ -38,17 +38,32 @@
 
     barrier = pltpu.get_barrier_semaphore()
 
-    def greet(axis, here, count):
-        def one(step, carry):
-            pl.semaphore_signal(
-                barrier, inc=1, device_id={axis: lax.rem(here + step, count)}, device_id_type=MESH
-            )
-            return carry
-        lax.fori_loop(1, count, one, 0)
-
-    greet("seq", me, n_seq)
-    greet("head", side, n_head)
-    pl.semaphore_wait(barrier, n_seq + n_head - 2)
+    def greet(where):
+        pl.semaphore_signal(barrier, inc=1, device_id=where, device_id_type=MESH)
+
+    above, below = (z + 1 < n_z).astype(jnp.int32), (z > 0).astype(jnp.int32)
+    loads = [
+        pltpu.make_async_copy(ref.at[c], own.at[c, k], own_sem.at[c, k])
+        for c in range(heads_kv) for k, ref in enumerate((k_hbm, v_hbm))
+    ]
+    for load in loads:
+        load.start()
+    q_load = pltpu.make_async_copy(q_hbm, q_ref, q_sem)
+    q_load.start()
+    greet({"seq": base + px})
+    greet({"seq": base + py})
+
+    @pl.when(z + 1 < n_z)
+    def _():
+        greet({"seq": me + PLANE})
+
+    @pl.when(z > 0)
+    def _():
+        greet({"seq": me - PLANE})
+
+    for step in range(1, n_head):
+        greet({"head": lax.rem(side + step, n_head)})
+    pl.semaphore_wait(barrier, n_head + 1 + above + below)
 
     def send(kind, src, plane, source, c, target):
         return pltpu.make_async_remote_copy(
@@ -69,16 +84,20 @@
     x_old, y_old, d_old = 2 * bit0, 2 * bit1, 2 * bit1
     x_from, y_from, d_from = 2 - 2 * bit0, 2 - 2 * bit1, 2 - 2 * bit1
 
-    def sink_copy(target):
+    def sink_copy(way, source, target):
         return pltpu.make_async_remote_copy(
-            src_ref=own.at[:, :, pl.ds(0, SINK_ROWS)],
+            src_ref=source,
             dst_ref=sink,
-            send_sem=sink_send.at[target],
+            send_sem=sink_send.at[way],
             recv_sem=sink_recv,
             device_id={"seq": target},
             device_id_type=MESH,
         )
 
+    first_rows = own.at[:, :, pl.ds(0, SINK_ROWS)]
+
+    for load in loads:
+        load.wait()
     for c in range(heads_kv):
         @pl.when(z + 1 < n_z)
         def _():
@@ -95,14 +114,17 @@
         if c == 0:
             @pl.when(me == 0)
             def _():
-                def one(target, carry):
-                    sink_copy(target).start()
-                    return carry
-                lax.fori_loop(1, n_seq, one, 0)
+                sink_copy(0, first_rows, base + px).start()
+                sink_copy(1, first_rows, base + py).start()
+
+                @pl.when(z + 1 < n_z)
+                def _():
+                    sink_copy(2, first_rows, me + PLANE).start()
 
     fetch = pltpu.make_async_copy(w_hbm, w, w_sem)
     fetch.start()
 
+    q_load.wait()
     column = lax.broadcasted_iota(jnp.int32, (1, lanes), 1)
     for c in range(heads_kv):
         window, count, bias, token = (jnp.zeros((1, lanes), t) for t in (jnp.int32, jnp.int32, jnp.float32, jnp.int32))
@@ -125,27 +147,33 @@
     def attend(block, c, shard, causal=False, sinks=False):
         keys, values = block[0], block[1]
         key_row = lax.broadcasted_iota(jnp.int32, (keys.shape[0], 1), 0)
-        for n in range(0, lanes, 256):
-            cols = slice(n, n + 256)
-            s = jnp.dot(keys, qt[c, :, cols], preferred_element_type=jnp.float32) * scale
+        step = min(256, lanes)
+        parts = [slice(n, n + step) for n in range(0, lanes, step)]
+        scores = [jnp.dot(keys, qt[c, :, cols], preferred_element_type=jnp.float32) for cols in parts]
+        turned = values.T
+        olds = [top[c, :, cols] for cols in parts]
+        weights, news, fades, sums = [], [], [], []
+        for s, old, cols in zip(scores, olds, parts):
+            s = s * scale
             if sinks:
                 s = jnp.where(key_row <= few[c, :, cols], s + lift[c, :, cols], HIDDEN)
             else:
                 seen = key_row > low[c, :, cols] - shard * rows
                 if causal:
-                    token = lax.rem(lax.broadcasted_iota(jnp.int32, (1, 256), 1) + n, rows)
-                    seen = seen & (key_row <= token)
+                    column = lax.broadcasted_iota(jnp.int32, (1, step), 1) + cols.start
+                    seen = seen & (key_row <= lax.rem(column, rows))
                 s = jnp.where(seen, s, HIDDEN)
-            old = top[c, :, cols]
             new = jnp.maximum(old, jnp.max(s, axis=0, keepdims=True))
             e = jnp.exp2(s - new)
-            fade = jnp.exp2(old - new)
+            weights.append(e.astype(jnp.bfloat16))
+            news.append(new)
+            fades.append(jnp.exp2(old - new))
+            sums.append(jnp.sum(e, axis=0, keepdims=True))
+        adds = [jnp.dot(turned, e, preferred_element_type=jnp.float32) for e in weights]
+        for new, fade, total, add, cols in zip(news, fades, sums, adds, parts):
             top[c, :, cols] = new
-            norm[c, :, cols] = norm[c, :, cols] * fade + jnp.sum(e, axis=0, keepdims=True)
-            acc[c, :, cols] = acc[c, :, cols] * fade + lax.dot_general(
-                values, e.astype(jnp.bfloat16), (((0,), (0,)), ((), ())),
-                preferred_element_type=jnp.float32,
-            )
+            norm[c, :, cols] = norm[c, :, cols] * fade + total
+            acc[c, :, cols] = acc[c, :, cols] * fade + add
 
     def each(body):
         def one(c, carry):
@@ -169,6 +197,23 @@
             attend(held(1, p, c), c, me - PLANE)
         each(first)
 
+    def pass_on():
+        sink_copy(0, sink, me).wait_recv()
+
+        @pl.when(me == 1)
+        def _():
+            sink_copy(1, sink, base + py).start()
+
+        @pl.when(z + 1 < n_z)
+        def _():
+            sink_copy(2, sink, me + PLANE).start()
+
+    @pl.when((me > 0) & (z <= 1))
+    def _():
+        pass_on()
+
+    @pl.when(z >= 1)
+    def _():
         def second(c):
             @pl.when(z >= 2)
             def _():
@@ -195,13 +240,16 @@
             attend(held(y_from, py, c), c, base - y_from * PLANE + py)
     each(relay)
 
+    @pl.when(z >= 2)
+    def _():
+        pass_on()
+
     @pl.when(me == 0)
     def _():
         each(lambda c: attend(own.at[c, :, pl.ds(0, SINK_ROWS)], c, 0, sinks=True))
 
     @pl.when(me > 0)
     def _():
-        sink_copy(me).wait_recv()
         each(lambda c: attend(sink.at[c], c, 0, sinks=True))
 
     @pl.when(z >= 2)
@@ -312,10 +360,15 @@
 
     @pl.when(me == 0)
     def _():
-        def one(target, carry):
-            sink_copy(target).wait_send()
-            return carry
-        lax.fori_loop(1, n_seq, one, 0)
+        sink_copy(0, sink, base + px).wait_send()
+
+    @pl.when(me <= 1)
+    def _():
+        sink_copy(1, sink, base + py).wait_send()
+
+    @pl.when(z + 1 < n_z)
+    def _():
+        sink_copy(2, sink, me + PLANE).wait_send()
 
     def gone(t, carry):
         for step in range(1, n_head):
@@ -331,7 +384,7 @@
     lanes = group * rows
     depth, model = out_weight.shape
     assert (WINDOW - 1) // rows + 1 == 2 * PLANE and n_seq % PLANE == 0
-    own = jnp.stack([key_rows, value_rows]).transpose(2, 0, 1, 3)
+    keys, values = key_rows.transpose(1, 0, 2), value_rows.transpose(1, 0, 2)
     q = queries.transpose(1, 0, 2).reshape(kv_heads, lanes, width)
     tile = min(512, model)
     tiles = model // tile
@@ -343,9 +396,11 @@
     return pl.pallas_call(
         functools.partial(kernel, n_seq, n_head, tile),
         out_shape=jax.ShapeDtypeStruct((share, model), bf16),
-        in_specs=[smem, smem, smem, vmem, vmem, pl.BlockSpec(memory_space=pl.ANY)],
+        in_specs=[smem, smem, smem] + [pl.BlockSpec(memory_space=pl.ANY)] * 4,
         out_specs=vmem,
         scratch_shapes=[
+            pltpu.VMEM((kv_heads, 2, rows, width), bf16),
+            pltpu.VMEM((kv_heads, lanes, width), bf16),
             pltpu.VMEM((3 * PLANE, kv_heads, 2, rows, width), bf16),
             pltpu.VMEM((kv_heads, 2, SINK_ROWS, width), bf16),
             pltpu.VMEM((kv_heads, width, lanes), bf16),
@@ -361,7 +416,9 @@
             pltpu.VMEM((tiles, n_head - 1, share, tile), bf16),
             dma((8, kv_heads)),
             dma((3 * PLANE, kv_heads)),
-            dma((n_seq,)),
+            dma((3,)),
+            dma,
+            dma((kv_heads, 2)),
             dma,
             dma,
             dma((tiles, n_head - 1)),
@@ -370,7 +427,7 @@
         compiler_params=pltpu.CompilerParams(
             collective_id=0, has_side_effects=True, vmem_limit_bytes=56 * 1024 * 1024
         ),
-    )(windows, sink_counts, sink_bias, own, q, out_weight)
+    )(windows, sink_counts, sink_bias, keys, values, q, out_weight)
 
 
 def solution(mesh):

time: 70.9 us -> 61.1 us (0.86)
  the two profiles are of different devices: /device:TPU:17 before, /device:TPU:27 now
where the time goes in v2:
time: 61.1 us; the launch traced here: 60.8 us
  Pallas kernels  54.7 us (90%)
  local copies, waits for them, and re-layouts  6.09 us (10%)
    pallas_call x1, Pallas kernels, shards(): pl.pallas_call(functools.partial(kernel, n_seq, n_head, tile), out_shape=...  54.7 us
    transpose x1, local copies, waits for them, and re-layouts, shards(): q = queries.transpose(1, 0, 2).reshape(kv_heads, lanes, width)  2.22 us
    unnamed x1, local copies, waits for them, and re-layouts  2.06 us
    transpose x1, local copies, waits for them, and re-layouts, shards(): keys, values = (key_rows.transpose(1, 0, 2), value_rows.transpose(1, 0, 2))  1.81 us

profile of v2, /device:TPU:27, one launch (start us, length us, event | category | flops | bytes accessed | tf_op | source)
XLA Modules:
  0.0 60.8 jit_solution(8233512695109763547)
XLA Ops:
  0.0 1.8 %copy_bitcast_fusion = (bf16[4,192,128]{2,1,0:T(8,128)(2,1)}, bf16[4,192,128]{2,1,0:T(8,128)(2,1)}) fusion(bf16[192,4,128]{2,1,0:T(4,128)(2,1)} %param.9, bf16[192,4,128]{2,1,0:T(4,128)(2,1)} %param.8), kind=kLoop, calls=%fused_computation | loop fusion | bytes 786432 | tf_op jit(solution)/shard_map/transpose | solution.py:387
  1.8 2.2 %copy.10 = bf16[16,192,128]{2,1,0:T(8,128)(2,1)} copy(bf16[16,192,128]{2,0,1:T(8,128)(2,1)} %bitcast.7) | data formatting | bytes 1572864 | tf_op jit(solution)/shard_map/transpose | solution.py:388
  4.0 54.7 %shard_map.73 = bf16[96,4096]{1,0:T(8,128)(2,1)} custom-call(s32[16]{0:T(128)} %win_ref.1, s32[16]{0:T(128)} %cnt_ref.1, f32[16]{0:T(128)} %bias_ref.1, bf16[4,192,128]{2,1,0:T(8,128)(2,1)} %get-tuple-element.6.k_hbm, bf16[4,192,128]{2,1,0:T(8,128)(2,1)} %get-tuple-element.5.v_hbm, bf16[4,768,128]{2,1,0:T(8,128)(2,1)} %bitcast.6, bf16[2048,4096]{1,0:T(8,128)(2,1)} %w_hbm.1), custom_call_target="tpu_custom_call" | custom-call | tf_op jit(solution)/shard_map/pallas_call | solution.py:396
  58.7 2.1 %copy.14 = bf16[96,4096]{1,0:T(8,128)(2,1)} copy(bf16[96,4096]{1,0:T(8,128)(2,1)} %shard_map.73) | data formatting | bytes 1572864
